TPU v7x, 32 devices: a whole 2x2x4 slice. The times are simulated.
32 devices in a mesh: seq: 8 (over z, x), head: 4 (over y, core).
Axes of the slice: x: 2, y: 2, z: 4, core: 2. Of those that a mesh axis runs over, the one named last changes fastest.
Arguments:
- queries: bfloat16 [8192, 1536], P('seq', 'head'), may hold values from -5 to 5
- key_vectors: bfloat16 [8192, 1536], P('seq', 'head'), may hold values from -5 to 5
- value_vectors: bfloat16 [8192, 1536], P('seq', 'head'), may hold values from -6 to 6
- out_grad: bfloat16 [8192, 1536], P('seq', 'head'), may hold values from -6 to 6
- gate_logit: float32 [12], P('head'), may hold values from -2 to 2
- doc_index: int32 [8], replicated, may hold values from 0 to 3, never falling along the last dimension, each value on 1 to 4 neighbouring positions
Outputs:
- query_grad: float32 [8192, 1536], P('seq', 'head')
- key_grad: float32 [8192, 1536], P('seq', 'head')
- value_grad: float32 [8192, 1536], P('seq', 'head')
- gate_grad: float32 [12], P('head')
Inputs may be any that keep to these rules, and one draw needn't show every extreme that they name: `doc_index`: never falls from one segment to the next; every document holds 1 to 4 segments, and one holds exactly 4.
All inputs are finite; a program needn't handle non-finite values.
Results may differ from a plain program's by a relative error of at most 0.0017.
The roundings to bfloat16 on the way count: a program that leaves them out, or rounds other values in their place, can miss the bound.
Values sent between devices are 32-bit elements; how exact they have to be, the bound alone decides.
A program may use at most 128 MiB of HBM per device.

v0:
```python
import functools
import math

import jax
import jax.numpy as jnp
from jax import lax
from jax.experimental import pallas as pl
from jax.experimental.pallas import tpu as pltpu
from jax.sharding import PartitionSpec as P

MESH = pl.DeviceIdType.MESH
F32 = jnp.float32
BF16 = jnp.bfloat16


def exp_low(x):
    return jnp.exp(jnp.minimum(x, 0.0))


def feature(x):
    return jnp.where(x > 0, x + 1.0, exp_low(x))


def slope(x):
    return jnp.where(x > 0, 1.0, exp_low(x))


def dot_nn(a, b):
    return lax.dot_general(a, b, (((1,), (0,)), ((), ())), preferred_element_type=F32)


def dot_nt(a, b):
    return lax.dot_general(a, b, (((1,), (1,)), ((), ())), preferred_element_type=F32)


def dot_tn(a, b):
    return lax.dot_general(a, b, (((0,), (0,)), ((), ())), preferred_element_type=F32)


def split(x):
    high = x.astype(BF16)
    return high, (x - high.astype(F32)).astype(BF16)


def kernel(
    n, steps, reach, heads, size, block,
    doc_hbm, logit_hbm, q_hbm, k_hbm, v_hbm, g_hbm,
    qo, ko, vo, later_o, norm_o, share_o, gate_o,
    doc_ref, logit_ref, q_ref, k_ref, v_ref, g_ref, load_sem,
    kf, qf, inv_den, s_buf, g_buf, k_turned, gate_rows, gate_all,
    norm_src, norm_got, norm_sum, mem_src, mem_got, mem_sum,
    norm_send, norm_recv, mem_send, mem_recv, gate_send, gate_recv,
):
    me = lax.axis_index("seq")
    rows = q_ref.shape[0]
    blocks = rows // block
    scale = size ** -0.5
    signs = (1, -1)
    loads = [
        pltpu.make_async_copy(source, target, load_sem.at[i])
        for i, (source, target) in enumerate((
            (k_hbm, k_ref), (v_hbm, v_ref), (q_hbm, q_ref), (g_hbm, g_ref),
            (doc_hbm, doc_ref), (logit_hbm, logit_ref),
        ))
    ]
    for i in (0, 4, 5, 1):
        loads[i].start()
    for other in range(1, n):
        pl.semaphore_signal(
            pltpu.get_barrier_semaphore(), inc=1,
            device_id={"seq": lax.rem(me + other, n)}, device_id_type=MESH,
        )

    def cols(h):
        return slice(h * size, (h + 1) * size)

    def part(i):
        return slice(i * block, (i + 1) * block)

    def share(h, width):
        return 1.0 / (1.0 + jnp.exp(-jnp.full((1, width), logit_ref[h], F32)))

    def can_send(way, dist):
        return me + dist < n if way == 0 else me >= dist

    def can_recv(way, dist):
        return me >= dist if way == 0 else me + dist < n

    def weight(way, dist):
        other = lax.rem(me - signs[way] * dist + n, n)
        return jnp.where(doc_ref[other] == doc_ref[me], 1.0, 0.0).astype(F32)

    def norm_copy(way, dist):
        return pltpu.make_async_remote_copy(
            src_ref=norm_src.at[way], dst_ref=norm_got.at[way, dist - 1],
            send_sem=norm_send.at[way, dist - 1], recv_sem=norm_recv.at[way, dist - 1],
            device_id={"seq": lax.rem(me + signs[way] * dist + n, n)}, device_id_type=MESH,
        )

    def mem_copy(way, step, h):
        dist = 1 << step
        return pltpu.make_async_remote_copy(
            src_ref=mem_src.at[way, step, h], dst_ref=mem_got.at[way, step, h],
            send_sem=mem_send.at[way, step, h], recv_sem=mem_recv.at[way, step, h],
            device_id={"seq": lax.rem(me + signs[way] * dist + n, n)}, device_id_type=MESH,
        )

    def gate_copy(other):
        return pltpu.make_async_remote_copy(
            src_ref=gate_rows, dst_ref=gate_all.at[me],
            send_sem=gate_send.at[other - 1], recv_sem=gate_recv.at[other - 1],
            device_id={"seq": lax.rem(me + other, n)}, device_id_type=MESH,
        )

    def send_norms(way):
        for dist in range(1, reach + 1):
            @pl.when(can_send(way, dist))
            def _():
                norm_copy(way, dist).start()

    def take_norms(way):
        norm_sum[way] = jnp.zeros_like(norm_sum[way])
        for dist in range(1, reach + 1):
            @pl.when(can_recv(way, dist))
            def _():
                norm_copy(way, dist).wait_recv()
                norm_sum[way] += weight(way, dist) * norm_got[way, dist - 1]

    def send_mem(way, step, h):
        @pl.when(can_send(way, 1 << step))
        def _():
            mem_copy(way, step, h).start()

    def take_mem(way, step, h):
        if step == 0:
            mem_sum[way, h] = jnp.zeros_like(mem_sum[way, h])

        @pl.when(can_recv(way, 1 << step))
        def _():
            mem_copy(way, step, h).wait_recv()
            mem_sum[way, h] += weight(way, 1 << step) * mem_got[way, step, h]

        if step + 1 < steps:
            mem_src[way, step + 1, h] = mem_src[way, 0, h] + mem_sum[way, h]
            send_mem(way, step + 1, h)

    def attention(h, fresh, wanted):
        hs = cols(h)
        local_share = 1.0 - share(h, block)
        factor = scale * math.log2(math.e)
        gate_total = jnp.zeros((1, block), F32)
        if 0 in wanted:
            k_turned[...] = k_ref[:, hs].T
        for i in wanted:
            q_i = q_ref[part(i), hs]
            g_i = g_ref[part(i), hs]
            top = jnp.full((1, block), -1e30, F32)
            for j in range(i + 1):
                tile = dot_nt(k_ref[part(j), hs], q_i)
                if j == i:
                    key_ids = lax.broadcasted_iota(jnp.int32, (block, block), 0)
                    query_ids = lax.broadcasted_iota(jnp.int32, (block, block), 1)
                    tile = jnp.where(key_ids <= query_ids, tile, -1e30)
                s_buf[part(j), :] = tile
                top = jnp.maximum(top, jnp.max(tile, axis=0, keepdims=True))
            total = jnp.zeros((1, block), F32)
            for j in range(i + 1):
                tile = jnp.exp2((s_buf[part(j), :] - top) * factor)
                s_buf[part(j), :] = tile
                total = total + jnp.sum(tile, axis=0, keepdims=True)
            inverse = 1.0 / total
            delta = jnp.zeros((1, block), F32)
            for j in range(i + 1):
                att = s_buf[part(j), :] * inverse
                low = att.astype(BF16)
                grad = dot_nt(v_ref[part(j), hs], g_i)
                s_buf[part(j), :] = att
                g_buf[part(j), :] = grad
                delta = delta + jnp.sum(grad * att, axis=0, keepdims=True)
                gate_total = gate_total + jnp.sum(grad * low.astype(F32), axis=0, keepdims=True)
                piece = dot_nn(low, g_i)
                if j == i:
                    vo[part(j), hs] = piece
                else:
                    vo[part(j), hs] += piece
            q_turned = jnp.zeros((size, block), F32)
            for j in range(i + 1):
                score = (s_buf[part(j), :] * ((g_buf[part(j), :] - delta) * local_share)).astype(BF16)
                piece = dot_nn(score, q_i)
                if j == i:
                    ko[part(j), hs] = piece
                else:
                    ko[part(j), hs] += piece
                q_turned = q_turned + dot_nn(k_turned[:, part(j)], score)
            q_local = q_turned.T * scale
            if fresh:
                qo[part(i), hs] = q_local
            else:
                qo[part(i), hs] += q_local
        row = gate_total[:, :size]
        for c in range(1, block // size):
            row = row + gate_total[:, c * size:(c + 1) * size]
        memory_share = share(h, size)
        row = row * (memory_share * (1.0 - memory_share))
        gate_rows[h:h + 1, :] -= row

    everything = tuple(range(blocks))
    first, last = everything[:-1], everything[-1:]
    gate_rows[...] = jnp.zeros_like(gate_rows)
    norm_src[...] = jnp.zeros_like(norm_src)
    loads[0].wait()
    loads[2].start()
    loads[3].start()
    for h in range(heads):
        hs = cols(h)
        norm = jnp.zeros((1, size), F32)
        for i in range(blocks):
            low = feature(k_ref[part(i), hs].astype(F32)).astype(BF16)
            kf[part(i), hs] = low
            norm = norm + jnp.sum(low.astype(F32), axis=0, keepdims=True)
        norm_src[0, h:h + 1, :] = norm
    for i in (4, 5, 1):
        loads[i].wait()
    pl.semaphore_wait(pltpu.get_barrier_semaphore(), n - 1)
    send_norms(0)
    for h in range(heads):
        mem_src[0, 0, h] = dot_tn(v_ref[:, cols(h)], kf[:, cols(h)])
        send_mem(0, 0, h)
    loads[2].wait()
    loads[3].wait()
    for h in range(heads):
        share_o[h:h + 1, :] = 1.0 - share(h, size)
        for i in range(blocks):
            qf[part(i), cols(h)] = feature(q_ref[part(i), cols(h)].astype(F32)).astype(BF16)
    attention(0, True, first)

    take_norms(0)
    for h in range(heads):
        hs = cols(h)
        memory_share = share(h, size)
        norm = norm_sum[0, h:h + 1, :]
        grad_memory = jnp.zeros((2 * size, size), F32)
        for i in range(blocks):
            low = qf[part(i), hs]
            den = 1.0 + jnp.sum(low.astype(F32) * norm, axis=1, keepdims=True)
            inv = jnp.broadcast_to(1.0 / den, (block, size))
            inv_den[h, part(i), :] = inv
            num_grad = g_ref[part(i), hs].astype(F32) * (inv * memory_share)
            grad_memory = grad_memory + dot_tn(jnp.concatenate(split(num_grad), axis=1), low)
        mem_src[1, 0, h] = grad_memory[:size] + grad_memory[size:]
        send_mem(1, 0, h)

    early = min(2, heads)
    for h in range(heads):
        take_mem(0, 0, h)
    attention(0, True, last)
    for h in range(1, early):
        attention(h, True, first)
    for h in range(heads):
        take_mem(1, 0, h)
    for step in range(1, steps - 1):
        for way in range(2):
            for h in range(heads):
                take_mem(way, step, h)
    for h in range(1, early):
        attention(h, True, last)

    for h in range(heads):
        take_mem(0, steps - 1, h)
        hs = cols(h)
        memory_share = share(h, size)
        norm = norm_sum[0, h:h + 1, :]
        high, rest = split(mem_sum[0, h])
        beside = jnp.concatenate([high, rest], axis=1)
        below = jnp.concatenate([high, rest], axis=0)
        grad_norm = jnp.zeros((1, size), F32)
        gate_row = jnp.zeros((1, size), F32)
        for i in range(blocks):
            low = qf[part(i), hs]
            g_i = g_ref[part(i), hs]
            inv = inv_den[h, part(i), :]
            read = dot_nt(jnp.concatenate([low, low], axis=1), beside) * inv
            product = g_i.astype(F32) * read
            gate_row = gate_row + jnp.sum(product, axis=0, keepdims=True)
            den_grad = -(inv * memory_share) * jnp.sum(product, axis=1, keepdims=True)
            grad_norm = grad_norm + jnp.sum(den_grad * low.astype(F32), axis=0, keepdims=True)
            extra = dot_nn(jnp.concatenate([g_i, g_i], axis=1), below) * (inv * memory_share)
            extra = (extra + den_grad * norm) * slope(q_ref[part(i), hs].astype(F32))
            if h < early:
                qo[part(i), hs] += extra
            else:
                qo[part(i), hs] = extra
        gate_rows[h:h + 1, :] += gate_row * (memory_share * (1.0 - memory_share))
        norm_src[1, h:h + 1, :] = grad_norm
    send_norms(1)
    for h in range(early, heads):
        attention(h, False, everything)
    for other in range(1, n):
        gate_copy(other).start()
    gate_all[me] = gate_rows[...]

    take_norms(1)
    norm_o[...] = norm_sum[1]
    for h in range(heads):
        take_mem(1, steps - 1, h)
        later_o[h] = mem_sum[1, h]
    for other in range(1, n):
        gate_copy(other).wait_recv()
    gates = gate_all[0]
    for other in range(1, n):
        gates = gates + gate_all[other]
    gate_o[...] = gates

    for other in range(1, n):
        gate_copy(other).wait_send()
    for way in range(2):
        for dist in range(1, reach + 1):
            @pl.when(can_send(way, dist))
            def _():
                norm_copy(way, dist).wait_send()
        for step in range(steps):
            @pl.when(can_send(way, 1 << step))
            def _():
                for h in range(heads):
                    mem_copy(way, step, h).wait_send()


def finish(
    heads, size, block,
    q_ref, ko, vo, later_ref, norm_ref, share_ref, gate_ref, k_ref, v_ref,
    q_hbm, k_hbm, v_hbm, gate_o, k_out, v_out, q_sem, k_sem, v_sem,
):
    rows = k_ref.shape[0]
    scale = size ** -0.5
    copies = [pltpu.make_async_copy(q_ref, q_hbm, q_sem)]
    copies[0].start()
    weights = []
    for h in range(heads):
        high, rest = split(later_ref[h])
        weights.append((jnp.concatenate([high, rest], axis=1), jnp.concatenate([high, rest], axis=0)))
    for i in range(rows // block):
        here = slice(i * block, (i + 1) * block)
        for h in range(heads):
            hs = slice(h * size, (h + 1) * size)
            beside, below = weights[h]
            v_i = v_ref[here, hs]
            k_i = k_ref[here, hs].astype(F32)
            low = feature(k_i).astype(BF16)
            extra = dot_nn(jnp.concatenate([v_i, v_i], axis=1), below) + norm_ref[h:h + 1, :]
            k_out[here, hs] = ko[here, hs] * scale + extra * slope(k_i)
            value = dot_nt(jnp.concatenate([low, low], axis=1), beside)
            v_out[here, hs] = vo[here, hs] * share_ref[h:h + 1, :] + value
        for source, target, sem in ((k_out, k_hbm, k_sem), (v_out, v_hbm, v_sem)):
            copy = pltpu.make_async_copy(source.at[here], target.at[here], sem.at[i])
            copy.start()
            copies.append(copy)
    for h in range(heads):
        gate_o[h] = jnp.sum(gate_ref[h:h + 1, :])
    for copy in copies:
        copy.wait()


def solution(mesh):
    n = mesh.shape["seq"]
    longest = max(n // 2, 2)
    steps = (longest - 1).bit_length()
    reach = longest - 1

    def per_device(queries, key_vectors, value_vectors, out_grad, gate_logit, doc_index):
        rows, width = queries.shape
        heads = gate_logit.shape[0]
        size = width // heads
        block = min(256, rows)
        wide = jax.ShapeDtypeStruct((rows, width), F32)
        vmem = pl.BlockSpec(memory_space=pltpu.VMEM)
        smem = pl.BlockSpec(memory_space=pltpu.SMEM)
        hbm = pl.BlockSpec(memory_space=pltpu.HBM)
        tall = -(-heads // 8) * 8
        dma = pltpu.SemaphoreType.DMA
        small = jax.ShapeDtypeStruct((tall, size), F32)
        local = pl.pallas_call(
            functools.partial(kernel, n, steps, reach, heads, size, block),
            out_shape=(wide, wide, wide, jax.ShapeDtypeStruct((heads, size, size), F32), small, small, small),
            in_specs=[hbm] * 6,
            out_specs=(vmem,) * 7,
            scratch_shapes=[
                pltpu.SMEM(doc_index.shape, jnp.int32),
                pltpu.SMEM(gate_logit.shape, F32),
                pltpu.VMEM((rows, width), BF16),
                pltpu.VMEM((rows, width), BF16),
                pltpu.VMEM((rows, width), BF16),
                pltpu.VMEM((rows, width), BF16),
                dma((6,)),
                pltpu.VMEM((rows, width), BF16),
                pltpu.VMEM((rows, width), BF16),
                pltpu.VMEM((heads, rows, size), F32),
                pltpu.VMEM((rows, block), F32),
                pltpu.VMEM((rows, block), F32),
                pltpu.VMEM((size, rows), BF16),
                pltpu.VMEM((tall, size), F32),
                pltpu.VMEM((n, tall, size), F32),
                pltpu.VMEM((2, tall, size), F32),
                pltpu.VMEM((2, reach, tall, size), F32),
                pltpu.VMEM((2, tall, size), F32),
                pltpu.VMEM((2, steps, heads, size, size), F32),
                pltpu.VMEM((2, steps, heads, size, size), F32),
                pltpu.VMEM((2, heads, size, size), F32),
                dma((2, reach)),
                dma((2, reach)),
                dma((2, steps, heads)),
                dma((2, steps, heads)),
                dma((n - 1,)),
                dma((n - 1,)),
            ],
            compiler_params=pltpu.CompilerParams(
                collective_id=0, has_side_effects=True, vmem_limit_bytes=28 * 1024 * 1024
            ),
            cost_estimate=pl.CostEstimate(
                flops=14 * heads * rows * rows * size, bytes_accessed=20 * rows * width,
                transcendentals=heads * rows * rows,
            ),
            name="segment_backward",
        )(*(pltpu.with_memory_space_constraint(x, pltpu.HBM) for x in (doc_index, gate_logit, queries, key_vectors, value_vectors, out_grad)))
        return pl.pallas_call(
            functools.partial(finish, heads, size, block),
            out_shape=(wide, wide, wide, jax.ShapeDtypeStruct((heads,), F32)),
            in_specs=[vmem] * 9,
            out_specs=(hbm, hbm, hbm, smem),
            scratch_shapes=[
                pltpu.VMEM((rows, width), F32),
                pltpu.VMEM((rows, width), F32),
                dma(()),
                dma((rows // block,)),
                dma((rows // block,)),
            ],
            compiler_params=pltpu.CompilerParams(vmem_limit_bytes=16 * 1024 * 1024),
            cost_estimate=pl.CostEstimate(
                flops=8 * rows * width * size, bytes_accessed=12 * rows * width,
                transcendentals=rows * width,
            ),
            name="segment_finish",
        )(*local, key_vectors, value_vectors)

    spec = P("seq", "head")
    return jax.shard_map(
        per_device, mesh=mesh, in_specs=(spec, spec, spec, spec, P("head"), P()),
        out_specs=(spec, spec, spec, P("head")), check_vma=False,
    )
```

profile of v0, /device:TPU:0, one launch (start us, length us, event | category | flops | bytes accessed | tf_op | source)
XLA Modules:
  0.0 32.7 jit_solution(13054200806598393524)
XLA Ops:
  0.6 0.0 copy-start.1
  0.6 0.0 copy-start
  0.7 28.7 %segment_backward.1 = (f32[1024,384]{1,0:T(8,128)S(1)}, f32[1024,384]{1,0:T(8,128)S(1)}, f32[1024,384]{1,0:T(8,128)S(1)}, f32[3,128,128]{2,1,0:T(8,128)S(1)}, f3...) custom-call(s32[8]{0:T(128)} %doc_hbm.1, f32[3]{0:T(128)} %logit_hbm.1, bf16[1024,384]{1,0:T(8,128)(2,1)} %q_hbm.1, ...), custom_call_target="tpu_custom_call" | custom-call | flops 5637144576 | bytes 7864320 | tf_op jit(solution)/shard_map/segment_backward/pallas_call | solution.py:381
  29.4 0.0 copy-done.1
  29.4 0.0 copy-done
  29.4 3.2 %segment_finish.1 = (f32[1024,384]{1,0:T(8,128)}, f32[1024,384]{1,0:T(8,128)}, f32[1024,384]{1,0:T(8,128)}, f32[3]{0:T(128)}) custom-call(f32[1024,384]{1,0:T(8,128)S(1)} %get-tuple-element.11.q_ref, f32[1024,384]{1,0:T(8,128)S(1)} %get-tuple-element.12.ko, f32[1024,384]{1,0:T(8,128)S(1)} %get-tuple-element.13.vo, ...), custom_call_target="tpu_custom_call" | custom-call | flops 402653184 | bytes 4718592 | tf_op jit(solution)/shard_map/segment_finish/pallas_call | solution.py:424
Async XLA Ops:
  0.6 28.7 %copy-start.1 = (bf16[1024,384]{1,0:T(8,128)(2,1)S(1)}, bf16[1024,384]{1,0:T(8,128)(2,1)}, u32[]{:S(2)}) copy-start(bf16[1024,384]{1,0:T(8,128)(2,1)} %v_ref.1) | copy-start | bytes 2359300
  0.6 28.7 %copy-start = (bf16[1024,384]{1,0:T(8,128)(2,1)S(1)}, bf16[1024,384]{1,0:T(8,128)(2,1)}, u32[]{:S(2)}) copy-start(bf16[1024,384]{1,0:T(8,128)(2,1)} %k_ref.1) | copy-start | bytes 2359300
where the time goes:
time: 32.9 us; the launch traced here: 32.7 us
  Pallas kernels  31.9 us (97%)
  between operations  0.83 us (3%)
    pallas_call x1, Pallas kernels, per_device(): pl.pallas_call(functools.partial(kernel, n, steps, reach, heads, size, bl...  28.7 us
    pallas_call x1, Pallas kernels, per_device(): pl.pallas_call(functools.partial(finish, heads, size, block), out_shape=(...  3.15 us

commit v1 on v0

v1 whole, which is shorter than its diff:
```python
import functools
import math

import jax
import jax.numpy as jnp
from jax import lax
from jax.experimental import pallas as pl
from jax.experimental.pallas import tpu as pltpu
from jax.sharding import PartitionSpec as P

MESH = pl.DeviceIdType.MESH
F32 = jnp.float32
BF16 = jnp.bfloat16


def slope(x):
    return jnp.exp(jnp.minimum(x, 0.0))


def dot_nn(a, b):
    return lax.dot_general(a, b, (((1,), (0,)), ((), ())), preferred_element_type=F32)


def dot_nt(a, b):
    return lax.dot_general(a, b, (((1,), (1,)), ((), ())), preferred_element_type=F32)


def dot_tn(a, b):
    return lax.dot_general(a, b, (((0,), (0,)), ((), ())), preferred_element_type=F32)


def split(x):
    high = x.astype(BF16)
    return high, (x - high.astype(F32)).astype(BF16)


def merged(*lists):
    order = []
    for which, items in enumerate(lists):
        for at, item in enumerate(items):
            order.append(((at + 0.5) / len(items), which, at, item))
    return [entry[3] for entry in sorted(order, key=lambda entry: entry[:3])]


def kernel(
    n, steps, reach, heads, size, block,
    doc_hbm, logit_hbm, q_hbm, k_hbm, v_hbm, g_hbm,
    qo, ko, vo, gate_o,
    doc_ref, logit_ref, q_ref, k_ref, v_ref, g_ref, load_sem,
    kf, qf, k_slope, q_slope, inv_den, s_buf, g_buf, k_turned, gate_rows, gate_all,
    norm_src, norm_got, norm_sum, mem_src, mem_got, mem_sum,
    norm_send, norm_recv, mem_send, mem_recv, gate_send, gate_recv, entered,
):
    me = lax.axis_index("seq")
    rows = q_ref.shape[0]
    blocks = rows // block
    scale = size ** -0.5
    factor = scale * math.log2(math.e)
    signs = (1, -1)
    barrier = pltpu.get_barrier_semaphore()
    loads = [
        pltpu.make_async_copy(source, target, load_sem.at[i])
        for i, (source, target) in enumerate((
            (k_hbm, k_ref), (v_hbm, v_ref), (q_hbm, q_ref), (g_hbm, g_ref),
            (doc_hbm, doc_ref), (logit_hbm, logit_ref),
        ))
    ]
    for i in (0, 4, 5, 1, 2, 3):
        loads[i].start()

    def peer(way, dist):
        return {"seq": lax.rem(me + signs[way] * dist + n, n)}

    def can_send(way, dist):
        return me + dist < n if way == 0 else me >= dist

    def can_recv(way, dist):
        return me >= dist if way == 0 else me + dist < n

    for dist in range(1, reach + 1):
        for way in range(2):
            @pl.when(can_send(way, dist))
            def _():
                pl.semaphore_signal(barrier, inc=1, device_id=peer(way, dist), device_id_type=MESH)

    def cols(h):
        return slice(h * size, (h + 1) * size)

    def part(i):
        return slice(i * block, (i + 1) * block)

    def share(h, width):
        return 1.0 / (1.0 + jnp.exp(-jnp.full((1, width), logit_ref[h], F32)))

    def weight(way, dist):
        other = lax.rem(me - signs[way] * dist + n, n)
        return jnp.where(doc_ref[other] == doc_ref[me], 1.0, 0.0).astype(F32)

    def norm_copy(way, dist):
        return pltpu.make_async_remote_copy(
            src_ref=norm_src.at[way], dst_ref=norm_got.at[way, dist - 1],
            send_sem=norm_send.at[way, dist - 1], recv_sem=norm_recv.at[way, dist - 1],
            device_id=peer(way, dist), device_id_type=MESH,
        )

    def mem_copy(way, step, h):
        return pltpu.make_async_remote_copy(
            src_ref=mem_src.at[way, step, h], dst_ref=mem_got.at[way, step, h],
            send_sem=mem_send.at[way, step, h], recv_sem=mem_recv.at[way, step, h],
            device_id=peer(way, 1 << step), device_id_type=MESH,
        )

    def gate_copy(other):
        return pltpu.make_async_remote_copy(
            src_ref=gate_rows, dst_ref=gate_all.at[me],
            send_sem=gate_send.at[other - 1], recv_sem=gate_recv.at[other - 1],
            device_id={"seq": lax.rem(me + other, n)}, device_id_type=MESH,
        )

    def tell(turn):
        for way in range(2):
            @pl.when(can_send(way, reach))
            def _():
                pl.semaphore_signal(entered.at[turn, way], inc=1, device_id=peer(way, reach), device_id_type=MESH)

    def hear(turn):
        for way in range(2):
            @pl.when(can_recv(way, reach))
            def _():
                pl.semaphore_wait(entered.at[turn, way], 1)

    def send_norms(way):
        for dist in range(1, reach + 1):
            @pl.when(can_send(way, dist))
            def _():
                norm_copy(way, dist).start()

    def take_norms(way):
        norm_sum[way] = jnp.zeros_like(norm_sum[way])
        for dist in range(1, reach + 1):
            @pl.when(can_recv(way, dist))
            def _():
                norm_copy(way, dist).wait_recv()
                norm_sum[way] += weight(way, dist) * norm_got[way, dist - 1]

    def send_mem(way, step, h):
        @pl.when(can_send(way, 1 << step))
        def _():
            mem_copy(way, step, h).start()

    def take_mem(way, step, h):
        if step == 0:
            mem_sum[way, h] = jnp.zeros_like(mem_sum[way, h])

        @pl.when(can_recv(way, 1 << step))
        def _():
            mem_copy(way, step, h).wait_recv()
            mem_sum[way, h] += weight(way, 1 << step) * mem_got[way, step, h]

        if step + 1 < steps:
            mem_src[way, step + 1, h] = mem_src[way, 0, h] + mem_sum[way, h]
            send_mem(way, step + 1, h)

    units = [(h, i) for h in range(heads) for i in range(blocks)]
    kept = [{} for _ in units]

    def scores(u):
        h, i = units[u]
        held = s_buf.at[u % 3]

        def tile(j):
            def run():
                if i == 0:
                    k_turned[h] = k_ref[:, cols(h)].T
                out = dot_nt(k_ref[part(j), cols(h)], q_ref[part(i), cols(h)])
                if j == i:
                    key_ids = lax.broadcasted_iota(jnp.int32, (block, block), 0)
                    query_ids = lax.broadcasted_iota(jnp.int32, (block, block), 1)
                    out = jnp.where(key_ids <= query_ids, out, -1e30)
                held[part(j), :] = out
                top = jnp.max(out, axis=0, keepdims=True)
                kept[u]["top"] = top if j == 0 else jnp.maximum(kept[u]["top"], top)
            return run

        return [tile(j) for j in range(i + 1)]

    def weights(u):
        h, i = units[u]
        held = s_buf.at[u % 3]
        grads = g_buf.at[u % 2]

        def raise_tile(j):
            def run():
                out = jnp.exp2((held[part(j), :] - kept[u]["top"]) * factor)
                held[part(j), :] = out
                total = jnp.sum(out, axis=0, keepdims=True)
                kept[u]["total"] = total if j == 0 else kept[u]["total"] + total
                if j == i:
                    kept[u]["inverse"] = 1.0 / kept[u]["total"]
            return run

        def grad_tile(j):
            def run():
                g_i = g_ref[part(i), cols(h)]
                grad = dot_nt(v_ref[part(j), cols(h)], g_i)
                grads[part(j), :] = grad
                out = held[part(j), :]
                low = (out * kept[u]["inverse"]).astype(BF16)
                delta = jnp.sum(grad * out, axis=0, keepdims=True)
                kept[u]["delta"] = delta if j == 0 else kept[u]["delta"] + delta
                piece = dot_nn(low, g_i)
                if j == i:
                    vo[part(j), cols(h)] = piece
                    kept[u]["delta"] = kept[u]["delta"] * kept[u]["inverse"]
                    kept[u]["scaled"] = kept[u]["inverse"] * (1.0 - share(h, block))
                else:
                    vo[part(j), cols(h)] += piece
            return run

        return [raise_tile(j) for j in range(i + 1)] + [grad_tile(j) for j in range(i + 1)]

    def grads(u):
        h, i = units[u]
        held = s_buf.at[u % 3]
        grads = g_buf.at[u % 2]

        def tile(j):
            def run():
                q_i = q_ref[part(i), cols(h)]
                score = held[part(j), :] * ((grads[part(j), :] - kept[u]["delta"]) * kept[u]["scaled"])
                score = score.astype(BF16)
                piece = dot_nn(score, q_i)
                if j == i:
                    ko[part(j), cols(h)] = piece
                else:
                    ko[part(j), cols(h)] += piece
                turned = dot_nn(k_turned[h, :, part(j)], score)
                kept[u]["turned"] = turned if j == 0 else kept[u]["turned"] + turned
                if j == i:
                    qo[part(i), cols(h)] = kept[u]["turned"].T * scale
            return run

        return [tile(j) for j in range(i + 1)]

    def attend(at):
        lists = []
        if 0 <= at - 2 < len(units):
            lists.append(grads(at - 2))
        if 0 <= at - 1 < len(units):
            lists.append(weights(at - 1))
        if at < len(units):
            lists.append(scores(at))
        for run in merged(*lists):
            run()

    def memory_grads():
        take_norms(0)
        for h in range(heads):
            hs = cols(h)
            norm = norm_sum[0, h:h + 1, :]
            both = jnp.zeros((size, 2 * size), F32)
            for i in range(blocks):
                low = qf[part(i), hs]
                den = 1.0 + jnp.sum(low.astype(F32) * norm, axis=1, keepdims=True)
                inv = jnp.broadcast_to(1.0 / den, (block, size))
                inv_den[h, part(i), :] = inv
                num = g_ref[part(i), hs].astype(F32) * inv
                both = both + dot_tn(low, jnp.concatenate(split(num), axis=1))
            mem_src[1, 0, h] = (both[:, :size] + both[:, size:]) * share(h, size)
            send_mem(1, 0, h)

    def read_memory(h):
        hs = cols(h)
        memory_share = share(h, size)
        norm = norm_sum[0, h:h + 1, :]
        memory = mem_sum[0, h]
        beside = jnp.concatenate(split(memory), axis=1)
        grad_norm = jnp.zeros((1, size), F32)
        for i in range(blocks):
            low = qf[part(i), hs].astype(F32)
            g_i = g_ref[part(i), hs]
            inv = inv_den[h, part(i), :]
            weighted = inv * memory_share
            turned = dot_nt(jnp.concatenate([g_i, g_i], axis=1), beside)
            product = jnp.sum(low * turned, axis=1, keepdims=True)
            den_grad = -(weighted * inv) * product
            grad_norm = grad_norm + jnp.sum(den_grad * low, axis=0, keepdims=True)
            qo[part(i), hs] += (turned * weighted + den_grad * norm) * q_slope[part(i), hs]
        norm_src[1, h:h + 1, :] = grad_norm
        row = jnp.sum(memory * mem_src[1, 0, h], axis=0, keepdims=True)
        gate_rows[h:h + 1, :] += row * (1.0 - memory_share)

    def local_gate(h):
        memory_share = share(h, size)
        row = jnp.zeros((1, size), F32)
        for i in range(blocks):
            row = row + jnp.sum(v_ref[part(i), cols(h)].astype(F32) * vo[part(i), cols(h)], axis=0, keepdims=True)
        gate_rows[h:h + 1, :] = -row * (memory_share * (1.0 - memory_share))

    def finish(h):
        hs = cols(h)
        local_share = 1.0 - share(h, size)
        high, rest = split(mem_sum[1, h])
        beside = jnp.concatenate([high, rest], axis=1)
        below = jnp.concatenate([high, rest], axis=0)
        for i in range(blocks):
            v_i = v_ref[part(i), hs]
            low = kf[part(i), hs]
            extra = dot_nt(jnp.concatenate([v_i, v_i], axis=1), beside)
            ko[part(i), hs] = ko[part(i), hs] * scale + extra * k_slope[part(i), hs]
            value = dot_nn(jnp.concatenate([low, low], axis=1), below)
            vo[part(i), hs] = vo[part(i), hs] * local_share + value

    gate_rows[...] = jnp.zeros_like(gate_rows)
    norm_src[...] = jnp.zeros_like(norm_src)
    loads[0].wait()
    for h in range(heads):
        norm = jnp.zeros((1, size), F32)
        for i in range(blocks):
            x = k_ref[part(i), cols(h)].astype(F32)
            flat = slope(x)
            k_slope[part(i), cols(h)] = flat
            low = (jnp.maximum(x, 0.0) + flat).astype(BF16)
            kf[part(i), cols(h)] = low
            norm = norm + jnp.sum(low.astype(F32), axis=0, keepdims=True)
        norm_src[0, h:h + 1, :] = norm
    for i in (4, 5, 1):
        loads[i].wait()
    for h in range(heads):
        mem_src[0, 0, h] = dot_tn(kf[:, cols(h)], v_ref[:, cols(h)])
    loads[2].wait()
    loads[3].wait()
    for h in range(heads):
        for i in range(blocks):
            x = q_ref[part(i), cols(h)].astype(F32)
            flat = slope(x)
            q_slope[part(i), cols(h)] = flat
            qf[part(i), cols(h)] = (jnp.maximum(x, 0.0) + flat).astype(BF16)
    pl.semaphore_wait(barrier, jnp.minimum(me, reach) + jnp.minimum(n - 1 - me, reach))
    send_norms(0)
    for h in range(heads):
        send_mem(0, 0, h)
    turns = -(-(n - 1) // reach) - 1
    if turns:
        tell(0)

    last = len(units) + 1
    polls = {}
    if steps > 1:
        order = [(0, 0), (0, 1), (1, 0), (0, 2), (1, 1), (1, 2)]
        order += [(way, h) for h in range(3, heads) for way in range(2)]
        order = [(way, h) for way, h in order if h < heads]
        for (way, h), at in zip(order, [4, 6, 7, 8, 9, 11] + [last] * len(order)):
            polls.setdefault(min(at, last), []).append((way, h))
    for at in range(last + 1):
        attend(at)
        if at == min(2, last):
            memory_grads()
        for way, h in polls.get(at, []):
            take_mem(way, 0, h)
        for turn in range(turns):
            if at == min(8 + 3 * turn, last):
                hear(turn)
                if turn + 1 < turns:
                    tell(turn + 1)
    for step in range(1, steps - 1):
        for h in range(heads):
            for way in range(2):
                take_mem(way, step, h)
    for h in range(heads):
        local_gate(h)
    for h in range(heads):
        take_mem(0, steps - 1, h)
        read_memory(h)
    send_norms(1)
    for other in range(1, n):
        gate_copy(other).start()
    gate_all[me] = gate_rows[...]
    for h in range(heads):
        take_mem(1, steps - 1, h)
        finish(h)
    take_norms(1)
    for h in range(heads):
        norm = norm_sum[1, h:h + 1, :]
        for i in range(blocks):
            ko[part(i), cols(h)] += norm * k_slope[part(i), cols(h)]
    for other in range(1, n):
        gate_copy(other).wait_recv()
    gates = gate_all[0]
    for other in range(1, n):
        gates = gates + gate_all[other]
    gate_o[...] = gates

    for other in range(1, n):
        gate_copy(other).wait_send()
    for way in range(2):
        for dist in range(1, reach + 1):
            @pl.when(can_send(way, dist))
            def _():
                norm_copy(way, dist).wait_send()
        for step in range(steps):
            @pl.when(can_send(way, 1 << step))
            def _():
                for h in range(heads):
                    mem_copy(way, step, h).wait_send()


def write(heads, q_ref, k_ref, v_ref, gate_ref, q_hbm, k_hbm, v_hbm, gate_o, sems):
    copies = [
        pltpu.make_async_copy(source, target, sems.at[i])
        for i, (source, target) in enumerate(((q_ref, q_hbm), (k_ref, k_hbm), (v_ref, v_hbm)))
    ]
    for copy in copies:
        copy.start()
    for h in range(heads):
        gate_o[h] = jnp.sum(gate_ref[h:h + 1, :])
    for copy in copies:
        copy.wait()


def solution(mesh):
    n = mesh.shape["seq"]
    longest = max(n // 2, 2)
    steps = (longest - 1).bit_length()
    reach = longest - 1

    def per_device(queries, key_vectors, value_vectors, out_grad, gate_logit, doc_index):
        rows, width = queries.shape
        heads = gate_logit.shape[0]
        size = width // heads
        block = min(256, rows)
        wide = jax.ShapeDtypeStruct((rows, width), F32)
        vmem = pl.BlockSpec(memory_space=pltpu.VMEM)
        smem = pl.BlockSpec(memory_space=pltpu.SMEM)
        hbm = pl.BlockSpec(memory_space=pltpu.HBM)
        tall = -(-heads // 8) * 8
        dma = pltpu.SemaphoreType.DMA
        local = pl.pallas_call(
            functools.partial(kernel, n, steps, reach, heads, size, block),
            out_shape=(wide, wide, wide, jax.ShapeDtypeStruct((tall, size), F32)),
            in_specs=[hbm] * 6,
            out_specs=(vmem,) * 4,
            scratch_shapes=[
                pltpu.SMEM(doc_index.shape, jnp.int32),
                pltpu.SMEM(gate_logit.shape, F32),
                pltpu.VMEM((rows, width), BF16),
                pltpu.VMEM((rows, width), BF16),
                pltpu.VMEM((rows, width), BF16),
                pltpu.VMEM((rows, width), BF16),
                dma((6,)),
                pltpu.VMEM((rows, width), BF16),
                pltpu.VMEM((rows, width), BF16),
                pltpu.VMEM((rows, width), F32),
                pltpu.VMEM((rows, width), F32),
                pltpu.VMEM((heads, rows, size), F32),
                pltpu.VMEM((3, rows, block), F32),
                pltpu.VMEM((2, rows, block), F32),
                pltpu.VMEM((heads, size, rows), BF16),
                pltpu.VMEM((tall, size), F32),
                pltpu.VMEM((n, tall, size), F32),
                pltpu.VMEM((2, tall, size), F32),
                pltpu.VMEM((2, reach, tall, size), F32),
                pltpu.VMEM((2, tall, size), F32),
                pltpu.VMEM((2, steps, heads, size, size), F32),
                pltpu.VMEM((2, steps, heads, size, size), F32),
                pltpu.VMEM((2, heads, size, size), F32),
                dma((2, reach)),
                dma((2, reach)),
                dma((2, steps, heads)),
                dma((2, steps, heads)),
                dma((n - 1,)),
                dma((n - 1,)),
                pltpu.SemaphoreType.REGULAR((-(-(n - 1) // reach), 2)),
            ],
            compiler_params=pltpu.CompilerParams(
                collective_id=0, has_side_effects=True, vmem_limit_bytes=40 * 1024 * 1024
            ),
            cost_estimate=pl.CostEstimate(
                flops=14 * heads * rows * rows * size, bytes_accessed=20 * rows * width,
                transcendentals=heads * rows * rows,
            ),
            name="segment_backward",
        )(*(pltpu.with_memory_space_constraint(x, pltpu.HBM) for x in (doc_index, gate_logit, queries, key_vectors, value_vectors, out_grad)))
        return pl.pallas_call(
            functools.partial(write, heads),
            out_shape=(wide, wide, wide, jax.ShapeDtypeStruct((heads,), F32)),
            in_specs=[vmem] * 4,
            out_specs=(hbm, hbm, hbm, smem),
            scratch_shapes=[dma((3,))],
            compiler_params=pltpu.CompilerParams(vmem_limit_bytes=16 * 1024 * 1024),
            cost_estimate=pl.CostEstimate(
                flops=8 * rows * width * size, bytes_accessed=12 * rows * width,
                transcendentals=rows * width,
            ),
            name="segment_finish",
        )(*local)

    spec = P("seq", "head")
    return jax.shard_map(
        per_device, mesh=mesh, in_specs=(spec, spec, spec, spec, P("head"), P()),
        out_specs=(spec, spec, spec, P("head")), check_vma=False,
    )
```

time: 32.9 us -> 27.5 us (0.84)
  Pallas kernels: 31.9 us -> 26.7 us
    pallas_call x1, Pallas kernels: 28.7 us -> 24 us  [per_device(): pl.pallas_call(functools.partial(kernel, n, steps, reach, heads, size, bl...]
    pallas_call x1, Pallas kernels: 3.15 us -> 2.72 us  [per_device(): pl.pallas_call(functools.partial(write, heads), out_shape=(wide, wide, wi...]
where the time goes in v1:
time: 27.5 us; the launch traced here: 27.3 us
  Pallas kernels  26.7 us (97%)
  between operations  0.64 us (2%)
    pallas_call x1, Pallas kernels, per_device(): pl.pallas_call(functools.partial(kernel, n, steps, reach, heads, size, bl...  24 us
    pallas_call x1, Pallas kernels, per_device(): pl.pallas_call(functools.partial(write, heads), out_shape=(wide, wide, wi...  2.72 us

profile of v1, /device:TPU:0, one launch (start us, length us, event | category | flops | bytes accessed | tf_op | source)
XLA Modules:
  0.0 27.3 jit_solution(4369338970414002387)
XLA Ops:
  0.6 24.0 %segment_backward.1 = (f32[1024,384]{1,0:T(8,128)S(1)}, f32[1024,384]{1,0:T(8,128)S(1)}, f32[1024,384]{1,0:T(8,128)S(1)}, f32[8,128]{1,0:T(8,128)S(1)}) custom-call(s32[8]{0:T(128)} %doc_hbm.1, f32[3]{0:T(128)} %logit_hbm.1, bf16[1024,384]{1,0:T(8,128)(2,1)} %q_hbm.1, bf16[1024,384]{1,0:T(8,128)(2,1)} %k_hbm.1, bf16[1024,384]{1,0:T(8,128)(2,1)} %v_hbm.1, ...), custom_call_target="tpu_custom_call" | custom-call | flops 5637144576 | bytes 7864320 | tf_op jit(solution)/shard_map/segment_backward/pallas_call | solution.py:438
  24.6 2.7 %segment_finish.1 = (f32[1024,384]{1,0:T(8,128)}, f32[1024,384]{1,0:T(8,128)}, f32[1024,384]{1,0:T(8,128)}, f32[3]{0:T(128)}) custom-call(f32[1024,384]{1,0:T(8,128)S(1)} %get-tuple-element.8.q_ref, f32[1024,384]{1,0:T(8,128)S(1)} %get-tuple-element.9.k_ref, f32[1024,384]{1,0:T(8,128)S(1)} %get-tuple-element.10.v_ref, f32[8,128]{1,0:T(8,128)S(1)} %get-tuple-element.11.gate_ref), custom_call_target="tpu_custom_call" | custom-call | flops 402653184 | bytes 4718592 | tf_op jit(solution)/shard_map/segment_finish/pallas_call | solution.py:484

commit v2 on v1

--- a/solution.py
+++ b/solution.py
@@ -47,7 +47,7 @@
     doc_hbm, logit_hbm, q_hbm, k_hbm, v_hbm, g_hbm,
     qo, ko, vo, gate_o,
     doc_ref, logit_ref, q_ref, k_ref, v_ref, g_ref, load_sem,
-    kf, qf, k_slope, q_slope, inv_den, s_buf, g_buf, k_turned, gate_rows, gate_all,
+    kf, qf, k_slope, q_slope, extra, inv_den, s_buf, g_buf, k_turned, gate_rows, gate_all,
     norm_src, norm_got, norm_sum, mem_src, mem_got, mem_sum,
     norm_send, norm_recv, mem_send, mem_recv, gate_send, gate_recv, entered,
 ):
@@ -113,7 +113,7 @@
     def gate_copy(other):
         return pltpu.make_async_remote_copy(
             src_ref=gate_rows, dst_ref=gate_all.at[me],
-            send_sem=gate_send.at[other - 1], recv_sem=gate_recv.at[other - 1],
+            send_sem=gate_send, recv_sem=gate_recv,
             device_id={"seq": lax.rem(me + other, n)}, device_id_type=MESH,
         )
 
@@ -242,60 +242,71 @@
 
         return [tile(j) for j in range(i + 1)]
 
-    def attend(at):
-        lists = []
+    def attend(at, *more):
+        lists = [items for items in more if items]
         if 0 <= at - 2 < len(units):
             lists.append(grads(at - 2))
         if 0 <= at - 1 < len(units):
             lists.append(weights(at - 1))
-        if at < len(units):
+        if 0 <= at < len(units):
             lists.append(scores(at))
         for run in merged(*lists):
             run()
 
-    def memory_grads():
-        take_norms(0)
-        for h in range(heads):
-            hs = cols(h)
-            norm = norm_sum[0, h:h + 1, :]
-            both = jnp.zeros((size, 2 * size), F32)
-            for i in range(blocks):
+    def memory_grads(h):
+        hs = cols(h)
+        held = {}
+
+        def rows_of(i):
+            def run():
+                norm = norm_sum[0, h:h + 1, :]
                 low = qf[part(i), hs]
                 den = 1.0 + jnp.sum(low.astype(F32) * norm, axis=1, keepdims=True)
                 inv = jnp.broadcast_to(1.0 / den, (block, size))
                 inv_den[h, part(i), :] = inv
                 num = g_ref[part(i), hs].astype(F32) * inv
-                both = both + dot_tn(low, jnp.concatenate(split(num), axis=1))
-            mem_src[1, 0, h] = (both[:, :size] + both[:, size:]) * share(h, size)
-            send_mem(1, 0, h)
+                both = dot_tn(low, jnp.concatenate(split(num), axis=1))
+                held["both"] = both if i == 0 else held["both"] + both
+                if i == blocks - 1:
+                    both = held["both"]
+                    mem_src[1, 0, h] = (both[:, :size] + both[:, size:]) * share(h, size)
+            return run
+
+        return [rows_of(i) for i in range(blocks)]
 
     def read_memory(h):
         hs = cols(h)
-        memory_share = share(h, size)
-        norm = norm_sum[0, h:h + 1, :]
-        memory = mem_sum[0, h]
-        beside = jnp.concatenate(split(memory), axis=1)
-        grad_norm = jnp.zeros((1, size), F32)
-        for i in range(blocks):
-            low = qf[part(i), hs].astype(F32)
-            g_i = g_ref[part(i), hs]
-            inv = inv_den[h, part(i), :]
-            weighted = inv * memory_share
-            turned = dot_nt(jnp.concatenate([g_i, g_i], axis=1), beside)
-            product = jnp.sum(low * turned, axis=1, keepdims=True)
-            den_grad = -(weighted * inv) * product
-            grad_norm = grad_norm + jnp.sum(den_grad * low, axis=0, keepdims=True)
-            qo[part(i), hs] += (turned * weighted + den_grad * norm) * q_slope[part(i), hs]
-        norm_src[1, h:h + 1, :] = grad_norm
-        row = jnp.sum(memory * mem_src[1, 0, h], axis=0, keepdims=True)
-        gate_rows[h:h + 1, :] += row * (1.0 - memory_share)
+        held = {}
+
+        def rows_of(i):
+            def run():
+                memory_share = share(h, size)
+                norm = norm_sum[0, h:h + 1, :]
+                beside = jnp.concatenate(split(mem_sum[0, h]), axis=1)
+                low = qf[part(i), hs].astype(F32)
+                g_i = g_ref[part(i), hs]
+                inv = inv_den[h, part(i), :]
+                weighted = inv * memory_share
+                turned = dot_nt(jnp.concatenate([g_i, g_i], axis=1), beside)
+                product = jnp.sum(low * turned, axis=1, keepdims=True)
+                den_grad = -(weighted * inv) * product
+                row = jnp.sum(den_grad * low, axis=0, keepdims=True)
+                held["row"] = row if i == 0 else held["row"] + row
+                extra[part(i), hs] = (turned * weighted + den_grad * norm) * q_slope[part(i), hs]
+                if i == blocks - 1:
+                    norm_src[1, h:h + 1, :] = held["row"]
+                    both = jnp.sum(mem_sum[0, h] * mem_src[1, 0, h], axis=0, keepdims=True)
+                    gate_rows[h:h + 1, :] += both * (1.0 - memory_share)
+            return run
+
+        return [rows_of(i) for i in range(blocks)]
 
     def local_gate(h):
         memory_share = share(h, size)
         row = jnp.zeros((1, size), F32)
         for i in range(blocks):
             row = row + jnp.sum(v_ref[part(i), cols(h)].astype(F32) * vo[part(i), cols(h)], axis=0, keepdims=True)
-        gate_rows[h:h + 1, :] = -row * (memory_share * (1.0 - memory_share))
+        gate_rows[h:h + 1, :] -= row * (memory_share * (1.0 - memory_share))
 
     def finish(h):
         hs = cols(h)
@@ -306,10 +317,27 @@
         for i in range(blocks):
             v_i = v_ref[part(i), hs]
             low = kf[part(i), hs]
-            extra = dot_nt(jnp.concatenate([v_i, v_i], axis=1), beside)
-            ko[part(i), hs] = ko[part(i), hs] * scale + extra * k_slope[part(i), hs]
+            turned = dot_nt(jnp.concatenate([v_i, v_i], axis=1), beside)
+            ko[part(i), hs] = ko[part(i), hs] * scale + turned * k_slope[part(i), hs]
             value = dot_nn(jnp.concatenate([low, low], axis=1), below)
             vo[part(i), hs] = vo[part(i), hs] * local_share + value
+            qo[part(i), hs] += extra[part(i), hs]
+
+    def key_memory(h):
+        def run():
+            mem_src[0, 0, h] = dot_tn(kf[:, cols(h)], v_ref[:, cols(h)])
+        return [run]
+
+    def query_features(h):
+        def rows_of(i):
+            def run():
+                x = q_ref[part(i), cols(h)].astype(F32)
+                flat = slope(x)
+                q_slope[part(i), cols(h)] = flat
+                qf[part(i), cols(h)] = (jnp.maximum(x, 0.0) + flat).astype(BF16)
+            return run
+
+        return [rows_of(i) for i in range(blocks)]
 
     gate_rows[...] = jnp.zeros_like(gate_rows)
     norm_src[...] = jnp.zeros_like(norm_src)
@@ -324,18 +352,9 @@
             kf[part(i), cols(h)] = low
             norm = norm + jnp.sum(low.astype(F32), axis=0, keepdims=True)
         norm_src[0, h:h + 1, :] = norm
-    for i in (4, 5, 1):
+    for i in (4, 5, 1, 2, 3):
         loads[i].wait()
-    for h in range(heads):
-        mem_src[0, 0, h] = dot_tn(kf[:, cols(h)], v_ref[:, cols(h)])
-    loads[2].wait()
-    loads[3].wait()
-    for h in range(heads):
-        for i in range(blocks):
-            x = q_ref[part(i), cols(h)].astype(F32)
-            flat = slope(x)
-            q_slope[part(i), cols(h)] = flat
-            qf[part(i), cols(h)] = (jnp.maximum(x, 0.0) + flat).astype(BF16)
+    attend(-1, *(key_memory(h) for h in range(heads)), *(query_features(h) for h in range(heads)))
     pl.semaphore_wait(barrier, jnp.minimum(me, reach) + jnp.minimum(n - 1 - me, reach))
     send_norms(0)
     for h in range(heads):
@@ -345,64 +364,74 @@
         tell(0)
 
     last = len(units) + 1
-    polls = {}
+    polls, reads = {}, {}
+    plan = []
     if steps > 1:
-        order = [(0, 0), (0, 1), (1, 0), (0, 2), (1, 1), (1, 2)]
-        order += [(way, h) for h in range(3, heads) for way in range(2)]
-        order = [(way, h) for way, h in order if h < heads]
-        for (way, h), at in zip(order, [4, 6, 7, 8, 9, 11] + [last] * len(order)):
-            polls.setdefault(min(at, last), []).append((way, h))
+        firsts = [(3, 0, 0), (4, 0, 1), (6, 0, 2), (7, 1, 0), (8, 1, 1), (9, 1, 2)]
+        plan += [(at, way, 0, h) for at, way, h in firsts if h < heads]
+        plan += [(last - 2, way, 0, h) for h in range(3, heads) for way in range(2)]
+    if steps == 2:
+        plan += [(9 + h, 0, 1, h) for h in range(min(heads, 3))]
+    for at, way, step, h in plan:
+        polls.setdefault(min(at, last - 1), []).append((way, step, h))
+        if way == 0 and step == steps - 1:
+            reads.setdefault(min(at, last - 1) + 1, []).append(h)
+    taken = [h for at in reads for h in reads[at]]
     for at in range(last + 1):
-        attend(at)
-        if at == min(2, last):
-            memory_grads()
-        for way, h in polls.get(at, []):
-            take_mem(way, 0, h)
-        for turn in range(turns):
-            if at == min(8 + 3 * turn, last):
+        grads_now = [memory_grads(h) for h in range(heads)] if at == 3 else []
+        if at == 3:
+            take_norms(0)
+        attend(at, *grads_now, *(read_memory(h) for h in reads.get(at, [])))
+        if at == 3:
+            for h in range(heads):
+                send_mem(1, 0, h)
+        for way, step, h in polls.get(at, []):
+            take_mem(way, step, h)
+        for turn in range(turns - 1):
+            if at == min(5 + 2 * turn, last):
                 hear(turn)
-                if turn + 1 < turns:
-                    tell(turn + 1)
+                tell(turn + 1)
     for step in range(1, steps - 1):
         for h in range(heads):
             for way in range(2):
                 take_mem(way, step, h)
     for h in range(heads):
+        if h not in taken:
+            take_mem(0, steps - 1, h)
+            attend(-1, read_memory(h))
+    send_norms(1)
+    for h in range(heads):
         local_gate(h)
-    for h in range(heads):
-        take_mem(0, steps - 1, h)
-        read_memory(h)
-    send_norms(1)
+    if turns:
+        hear(turns - 1)
     for other in range(1, n):
         gate_copy(other).start()
     gate_all[me] = gate_rows[...]
     for h in range(heads):
         take_mem(1, steps - 1, h)
         finish(h)
+    for way in range(2):
+        for dist in range(1, reach + 1):
+            @pl.when(can_send(way, dist))
+            def _():
+                norm_copy(way, dist).wait_send()
+        for step in range(steps):
+            @pl.when(can_send(way, 1 << step))
+            def _():
+                for h in range(heads):
+                    mem_copy(way, step, h).wait_send()
     take_norms(1)
     for h in range(heads):
         norm = norm_sum[1, h:h + 1, :]
         for i in range(blocks):
             ko[part(i), cols(h)] += norm * k_slope[part(i), cols(h)]
-    for other in range(1, n):
-        gate_copy(other).wait_recv()
+    others = gate_all.at[pl.ds(0, n - 1)]
+    pltpu.make_async_copy(others, others, gate_recv).wait()
     gates = gate_all[0]
     for other in range(1, n):
         gates = gates + gate_all[other]
     gate_o[...] = gates
-
-    for other in range(1, n):
-        gate_copy(other).wait_send()
-    for way in range(2):
-        for dist in range(1, reach + 1):
-            @pl.when(can_send(way, dist))
-            def _():
-                norm_copy(way, dist).wait_send()
-        for step in range(steps):
-            @pl.when(can_send(way, 1 << step))
-            def _():
-                for h in range(heads):
-                    mem_copy(way, step, h).wait_send()
+    pltpu.make_async_copy(others, others, gate_send).wait()
 
 
 def write(heads, q_ref, k_ref, v_ref, gate_ref, q_hbm, k_hbm, v_hbm, gate_o, sems):
@@ -452,6 +481,7 @@
                 pltpu.VMEM((rows, width), BF16),
                 pltpu.VMEM((rows, width), F32),
                 pltpu.VMEM((rows, width), F32),
+                pltpu.VMEM((rows, width), F32),
                 pltpu.VMEM((heads, rows, size), F32),
                 pltpu.VMEM((3, rows, block), F32),
                 pltpu.VMEM((2, rows, block), F32),
@@ -468,8 +498,8 @@
                 dma((2, reach)),
                 dma((2, steps, heads)),
                 dma((2, steps, heads)),
-                dma((n - 1,)),
-                dma((n - 1,)),
+                dma(()),
+                dma(()),
                 pltpu.SemaphoreType.REGULAR((-(-(n - 1) // reach), 2)),
             ],
             compiler_params=pltpu.CompilerParams(

time: 27.5 us -> 27.1 us (0.985)
  Pallas kernels: 26.7 us -> 26.3 us
    pallas_call x1, Pallas kernels: 24 us -> 23.6 us  [per_device(): pl.pallas_call(functools.partial(kernel, n, steps, reach, heads, size, bl...]
where the time goes in v2:
time: 27.1 us; the launch traced here: 26.9 us
  Pallas kernels  26.3 us (97%)
  between operations  0.64 us (2%)
    pallas_call x1, Pallas kernels, per_device(): pl.pallas_call(functools.partial(kernel, n, steps, reach, heads, size, bl...  23.6 us
    pallas_call x1, Pallas kernels, per_device(): pl.pallas_call(functools.partial(write, heads), out_shape=(wide, wide, wi...  2.72 us

profile of v2, /device:TPU:0, one launch (start us, length us, event | category | flops | bytes accessed | tf_op | source)
XLA Modules:
  0.0 26.9 jit_solution(16195957986859758605)
XLA Ops:
  0.6 23.6 %segment_backward.1 = (f32[1024,384]{1,0:T(8,128)S(1)}, f32[1024,384]{1,0:T(8,128)S(1)}, f32[1024,384]{1,0:T(8,128)S(1)}, f32[8,128]{1,0:T(8,128)S(1)}) custom-call(s32[8]{0:T(128)} %doc_hbm.1, f32[3]{0:T(128)} %logit_hbm.1, bf16[1024,384]{1,0:T(8,128)(2,1)} %q_hbm.1, bf16[1024,384]{1,0:T(8,128)(2,1)} %k_hbm.1, bf16[1024,384]{1,0:T(8,128)(2,1)} %v_hbm.1, ...), custom_call_target="tpu_custom_call" | custom-call | flops 5637144576 | bytes 7864320 | tf_op jit(solution)/shard_map/segment_backward/pallas_call | solution.py:467
  24.2 2.7 %segment_finish.1 = (f32[1024,384]{1,0:T(8,128)}, f32[1024,384]{1,0:T(8,128)}, f32[1024,384]{1,0:T(8,128)}, f32[3]{0:T(128)}) custom-call(f32[1024,384]{1,0:T(8,128)S(1)} %get-tuple-element.8.q_ref, f32[1024,384]{1,0:T(8,128)S(1)} %get-tuple-element.9.k_ref, f32[1024,384]{1,0:T(8,128)S(1)} %get-tuple-element.10.v_ref, f32[8,128]{1,0:T(8,128)S(1)} %get-tuple-element.11.gate_ref), custom_call_target="tpu_custom_call" | custom-call | flops 402653184 | bytes 4718592 | tf_op jit(solution)/shard_map/segment_finish/pallas_call | solution.py:514

commit v3 on v2

--- a/solution.py
+++ b/solution.py
@@ -106,7 +106,7 @@
     def mem_copy(way, step, h):
         return pltpu.make_async_remote_copy(
             src_ref=mem_src.at[way, step, h], dst_ref=mem_got.at[way, step, h],
-            send_sem=mem_send.at[way, step, h], recv_sem=mem_recv.at[way, step, h],
+            send_sem=mem_send.at[way, step], recv_sem=mem_recv.at[way, step, h],
             device_id=peer(way, 1 << step), device_id_type=MESH,
         )
 
@@ -302,11 +302,19 @@
         return [rows_of(i) for i in range(blocks)]
 
     def local_gate(h):
-        memory_share = share(h, size)
-        row = jnp.zeros((1, size), F32)
-        for i in range(blocks):
-            row = row + jnp.sum(v_ref[part(i), cols(h)].astype(F32) * vo[part(i), cols(h)], axis=0, keepdims=True)
-        gate_rows[h:h + 1, :] -= row * (memory_share * (1.0 - memory_share))
+        held = {}
+
+        def rows_of(i):
+            def run():
+                product = v_ref[part(i), cols(h)].astype(F32) * vo[part(i), cols(h)]
+                row = jnp.sum(product, axis=0, keepdims=True)
+                held["row"] = row if i == 0 else held["row"] + row
+                if i == blocks - 1:
+                    memory_share = share(h, size)
+                    gate_rows[h:h + 1, :] -= held["row"] * (memory_share * (1.0 - memory_share))
+            return run
+
+        return [rows_of(i) for i in range(blocks)]
 
     def finish(h):
         hs = cols(h)
@@ -367,30 +375,37 @@
     polls, reads = {}, {}
     plan = []
     if steps > 1:
-        firsts = [(3, 0, 0), (4, 0, 1), (6, 0, 2), (7, 1, 0), (8, 1, 1), (9, 1, 2)]
+        firsts = [(5, 0, 0), (7, 0, 1), (9, 0, 2), (10, 1, 0), (11, 1, 1), (12, 1, 2)]
         plan += [(at, way, 0, h) for at, way, h in firsts if h < heads]
         plan += [(last - 2, way, 0, h) for h in range(3, heads) for way in range(2)]
     if steps == 2:
-        plan += [(9 + h, 0, 1, h) for h in range(min(heads, 3))]
+        plan = [(10 + h, 0, 1, h) for h in range(min(heads, 3))] + plan
     for at, way, step, h in plan:
         polls.setdefault(min(at, last - 1), []).append((way, step, h))
         if way == 0 and step == steps - 1:
             reads.setdefault(min(at, last - 1) + 1, []).append(h)
     taken = [h for at in reads for h in reads[at]]
+    begin = min(5, last - 1)
     for at in range(last + 1):
-        grads_now = [memory_grads(h) for h in range(heads)] if at == 3 else []
-        if at == 3:
+        grads_now = [memory_grads(at - begin)] if begin < at < begin + heads else []
+        parts = grads_now + [read_memory(h) for h in reads.get(at, [])]
+        parts += [local_gate(h) for h in range(heads) if at == (h + 1) * blocks + 1]
+        attend(at, *parts)
+        if grads_now:
+            send_mem(1, 0, at - begin)
+        if at == begin:
             take_norms(0)
-        attend(at, *grads_now, *(read_memory(h) for h in reads.get(at, [])))
-        if at == 3:
-            for h in range(heads):
-                send_mem(1, 0, h)
+            attend(-1, memory_grads(0))
+            send_mem(1, 0, 0)
         for way, step, h in polls.get(at, []):
             take_mem(way, step, h)
         for turn in range(turns - 1):
-            if at == min(5 + 2 * turn, last):
+            if at == min(6 + 2 * turn, last):
                 hear(turn)
                 tell(turn + 1)
+    for h in range(last - begin + 1, heads):
+        attend(-1, memory_grads(h))
+        send_mem(1, 0, h)
     for step in range(1, steps - 1):
         for h in range(heads):
             for way in range(2):
@@ -400,8 +415,6 @@
             take_mem(0, steps - 1, h)
             attend(-1, read_memory(h))
     send_norms(1)
-    for h in range(heads):
-        local_gate(h)
     if turns:
         hear(turns - 1)
     for other in range(1, n):
@@ -418,8 +431,7 @@
         for step in range(steps):
             @pl.when(can_send(way, 1 << step))
             def _():
-                for h in range(heads):
-                    mem_copy(way, step, h).wait_send()
+                pltpu.make_async_copy(mem_src.at[way, step], mem_src.at[way, step], mem_send.at[way, step]).wait()
     take_norms(1)
     for h in range(heads):
         norm = norm_sum[1, h:h + 1, :]
@@ -496,11 +508,11 @@
                 pltpu.VMEM((2, heads, size, size), F32),
                 dma((2, reach)),
                 dma((2, reach)),
-                dma((2, steps, heads)),
+                dma((2, steps)),
                 dma((2, steps, heads)),
                 dma(()),
                 dma(()),
-                pltpu.SemaphoreType.REGULAR((-(-(n - 1) // reach), 2)),
+                pltpu.SemaphoreType.REGULAR((max(-(-(n - 1) // reach) - 1, 1), 2)),
             ],
             compiler_params=pltpu.CompilerParams(
                 collective_id=0, has_side_effects=True, vmem_limit_bytes=40 * 1024 * 1024

time: 27.1 us -> 26.7 us (0.985)
  Pallas kernels: 26.3 us -> 25.9 us
    pallas_call x1, Pallas kernels: 23.6 us -> 23.2 us  [per_device(): pl.pallas_call(functools.partial(kernel, n, steps, reach, heads, size, bl...]
where the time goes in v3:
time: 26.7 us; the launch traced here: 26.5 us
  Pallas kernels  25.9 us (97%)
  between operations  0.64 us (2%)
    pallas_call x1, Pallas kernels, per_device(): pl.pallas_call(functools.partial(kernel, n, steps, reach, heads, size, bl...  23.2 us
    pallas_call x1, Pallas kernels, per_device(): pl.pallas_call(functools.partial(write, heads), out_shape=(wide, wide, wi...  2.72 us

profile of v3, /device:TPU:0, one launch (start us, length us, event | category | flops | bytes accessed | tf_op | source)
XLA Modules:
  0.0 26.5 jit_solution(15348897972918496715)
XLA Ops:
  0.6 23.2 %segment_backward.1 = (f32[1024,384]{1,0:T(8,128)S(1)}, f32[1024,384]{1,0:T(8,128)S(1)}, f32[1024,384]{1,0:T(8,128)S(1)}, f32[8,128]{1,0:T(8,128)S(1)}) custom-call(s32[8]{0:T(128)} %doc_hbm.1, f32[3]{0:T(128)} %logit_hbm.1, bf16[1024,384]{1,0:T(8,128)(2,1)} %q_hbm.1, bf16[1024,384]{1,0:T(8,128)(2,1)} %k_hbm.1, bf16[1024,384]{1,0:T(8,128)(2,1)} %v_hbm.1, ...), custom_call_target="tpu_custom_call" | custom-call | flops 5637144576 | bytes 7864320 | tf_op jit(solution)/shard_map/segment_backward/pallas_call | solution.py:479
  23.8 2.7 %segment_finish.1 = (f32[1024,384]{1,0:T(8,128)}, f32[1024,384]{1,0:T(8,128)}, f32[1024,384]{1,0:T(8,128)}, f32[3]{0:T(128)}) custom-call(f32[1024,384]{1,0:T(8,128)S(1)} %get-tuple-element.8.q_ref, f32[1024,384]{1,0:T(8,128)S(1)} %get-tuple-element.9.k_ref, f32[1024,384]{1,0:T(8,128)S(1)} %get-tuple-element.10.v_ref, f32[8,128]{1,0:T(8,128)S(1)} %get-tuple-element.11.gate_ref), custom_call_target="tpu_custom_call" | custom-call | flops 402653184 | bytes 4718592 | tf_op jit(solution)/shard_map/segment_finish/pallas_call | solution.py:526

commit v4 on v3

--- a/solution.py
+++ b/solution.py
@@ -295,11 +295,20 @@
                 extra[part(i), hs] = (turned * weighted + den_grad * norm) * q_slope[part(i), hs]
                 if i == blocks - 1:
                     norm_src[1, h:h + 1, :] = held["row"]
-                    both = jnp.sum(mem_sum[0, h] * mem_src[1, 0, h], axis=0, keepdims=True)
-                    gate_rows[h:h + 1, :] += both * (1.0 - memory_share)
             return run
 
         return [rows_of(i) for i in range(blocks)]
+
+    def memory_gate(h):
+        both = jnp.sum(mem_sum[0, h] * mem_src[1, 0, h], axis=0, keepdims=True)
+        gate_rows[h:h + 1, :] += both * (1.0 - share(h, size))
+
+    def send_gates():
+        if turns:
+            hear(turns - 1)
+        for other in range(1, n):
+            gate_copy(other).start()
+        gate_all[me] = gate_rows[...]
 
     def local_gate(h):
         held = {}
@@ -347,6 +356,7 @@
 
         return [rows_of(i) for i in range(blocks)]
 
+    turns = -(-(n - 1) // reach) - 1
     gate_rows[...] = jnp.zeros_like(gate_rows)
     norm_src[...] = jnp.zeros_like(norm_src)
     loads[0].wait()
@@ -367,31 +377,25 @@
     send_norms(0)
     for h in range(heads):
         send_mem(0, 0, h)
-    turns = -(-(n - 1) // reach) - 1
     if turns:
         tell(0)
 
     last = len(units) + 1
-    polls, reads = {}, {}
-    plan = []
-    if steps > 1:
-        firsts = [(5, 0, 0), (7, 0, 1), (9, 0, 2), (10, 1, 0), (11, 1, 1), (12, 1, 2)]
-        plan += [(at, way, 0, h) for at, way, h in firsts if h < heads]
-        plan += [(last - 2, way, 0, h) for h in range(3, heads) for way in range(2)]
-    if steps == 2:
-        plan = [(10 + h, 0, 1, h) for h in range(min(heads, 3))] + plan
-    for at, way, step, h in plan:
-        polls.setdefault(min(at, last - 1), []).append((way, step, h))
-        if way == 0 and step == steps - 1:
-            reads.setdefault(min(at, last - 1) + 1, []).append(h)
-    taken = [h for at in reads for h in reads[at]]
-    begin = min(5, last - 1)
+    early = steps == 2 and heads == 3 and blocks == 4
+    if early:
+        polls = {6: [(0, 0, 0)], 8: [(0, 0, 1)], 9: [(0, 0, 2)], 10: [(0, 1, 0)], 11: [(0, 1, 1), (1, 0, 0)], 12: [(0, 1, 2)]}
+        reads = {11: [0], 13: [1, 2]}
+        late = [(1, 0, 1), (1, 0, 2)]
+    else:
+        polls, reads = {}, {}
+        late = [(way, step, h) for step in range(steps - 1) for h in range(heads) for way in range(2)]
+    begin = min(6, last - 1)
     for at in range(last + 1):
-        grads_now = [memory_grads(at - begin)] if begin < at < begin + heads else []
-        parts = grads_now + [read_memory(h) for h in reads.get(at, [])]
-        parts += [local_gate(h) for h in range(heads) if at == (h + 1) * blocks + 1]
+        parts = [memory_grads(at - begin)] if begin < at < begin + heads else []
+        parts += [read_memory(h) for h in reads.get(at, [])]
+        parts += [local_gate(h) for h in range(heads - 1) if at == (h + 1) * blocks + 1]
         attend(at, *parts)
-        if grads_now:
+        if begin < at < begin + heads:
             send_mem(1, 0, at - begin)
         if at == begin:
             take_norms(0)
@@ -399,27 +403,31 @@
             send_mem(1, 0, 0)
         for way, step, h in polls.get(at, []):
             take_mem(way, step, h)
+            if (way, step) == (0, steps - 1):
+                memory_gate(h)
         for turn in range(turns - 1):
-            if at == min(6 + 2 * turn, last):
+            if at == min(7 + 2 * turn, last):
                 hear(turn)
                 tell(turn + 1)
+        if at == last - 1:
+            attend(-1, local_gate(heads - 1))
+            if early:
+                send_gates()
+                take_mem(*late.pop(0))
     for h in range(last - begin + 1, heads):
         attend(-1, memory_grads(h))
         send_mem(1, 0, h)
-    for step in range(1, steps - 1):
+    if early:
+        send_norms(1)
+    for way, step, h in late:
+        take_mem(way, step, h)
+    if not early:
         for h in range(heads):
-            for way in range(2):
-                take_mem(way, step, h)
-    for h in range(heads):
-        if h not in taken:
             take_mem(0, steps - 1, h)
+            memory_gate(h)
             attend(-1, read_memory(h))
-    send_norms(1)
-    if turns:
-        hear(turns - 1)
-    for other in range(1, n):
-        gate_copy(other).start()
-    gate_all[me] = gate_rows[...]
+        send_norms(1)
+        send_gates()
     for h in range(heads):
         take_mem(1, steps - 1, h)
         finish(h)

time: 26.7 us -> 24.4 us (0.914)
  Pallas kernels: 25.9 us -> 23.6 us
    pallas_call x1, Pallas kernels: 23.2 us -> 20.9 us  [per_device(): pl.pallas_call(functools.partial(kernel, n, steps, reach, heads, size, bl...]
where the time goes in v4:
time: 24.4 us; the launch traced here: 24.3 us
  Pallas kernels  23.6 us (97%)
  between operations  0.64 us (3%)
    pallas_call x1, Pallas kernels, per_device(): pl.pallas_call(functools.partial(kernel, n, steps, reach, heads, size, bl...  20.9 us
    pallas_call x1, Pallas kernels, per_device(): pl.pallas_call(functools.partial(write, heads), out_shape=(wide, wide, wi...  2.72 us

profile of v4, /device:TPU:0, one launch (start us, length us, event | category | flops | bytes accessed | tf_op | source)
XLA Modules:
  0.0 24.3 jit_solution(3597048933584306879)
XLA Ops:
  0.6 20.9 %segment_backward.1 = (f32[1024,384]{1,0:T(8,128)S(1)}, f32[1024,384]{1,0:T(8,128)S(1)}, f32[1024,384]{1,0:T(8,128)S(1)}, f32[8,128]{1,0:T(8,128)S(1)}) custom-call(s32[8]{0:T(128)} %doc_hbm.1, f32[3]{0:T(128)} %logit_hbm.1, bf16[1024,384]{1,0:T(8,128)(2,1)} %q_hbm.1, bf16[1024,384]{1,0:T(8,128)(2,1)} %k_hbm.1, bf16[1024,384]{1,0:T(8,128)(2,1)} %v_hbm.1, ...), custom_call_target="tpu_custom_call" | custom-call | flops 5637144576 | bytes 7864320 | tf_op jit(solution)/shard_map/segment_backward/pallas_call | solution.py:487
  21.6 2.7 %segment_finish.1 = (f32[1024,384]{1,0:T(8,128)}, f32[1024,384]{1,0:T(8,128)}, f32[1024,384]{1,0:T(8,128)}, f32[3]{0:T(128)}) custom-call(f32[1024,384]{1,0:T(8,128)S(1)} %get-tuple-element.8.q_ref, f32[1024,384]{1,0:T(8,128)S(1)} %get-tuple-element.9.k_ref, f32[1024,384]{1,0:T(8,128)S(1)} %get-tuple-element.10.v_ref, f32[8,128]{1,0:T(8,128)S(1)} %get-tuple-element.11.gate_ref), custom_call_target="tpu_custom_call" | custom-call | flops 402653184 | bytes 4718592 | tf_op jit(solution)/shard_map/segment_finish/pallas_call | solution.py:534

commit v5 on v4

--- a/solution.py
+++ b/solution.py
@@ -45,14 +45,15 @@
 def kernel(
     n, steps, reach, heads, size, block,
     doc_hbm, logit_hbm, q_hbm, k_hbm, v_hbm, g_hbm,
-    qo, ko, vo, gate_o,
-    doc_ref, logit_ref, q_ref, k_ref, v_ref, g_ref, load_sem,
-    kf, qf, k_slope, q_slope, extra, inv_den, s_buf, g_buf, k_turned, gate_rows, gate_all,
+    qo, ko, vo, gate_o, later_o, norm_o, share_o, k_slope, kf, held_ref,
+    doc_ref, logit_ref, k_ref, load_sem,
+    qf, q_slope, extra, inv_den, s_buf, g_buf, k_turned, gate_rows, gate_all,
     norm_src, norm_got, norm_sum, mem_src, mem_got, mem_sum,
     norm_send, norm_recv, mem_send, mem_recv, gate_send, gate_recv, entered,
 ):
     me = lax.axis_index("seq")
-    rows = q_ref.shape[0]
+    v_ref, q_ref, g_ref = held_ref.at[0], held_ref.at[1], held_ref.at[2]
+    rows = k_ref.shape[0]
     blocks = rows // block
     scale = size ** -0.5
     factor = scale * math.log2(math.e)
@@ -60,13 +61,13 @@
     barrier = pltpu.get_barrier_semaphore()
     loads = [
         pltpu.make_async_copy(source, target, load_sem.at[i])
-        for i, (source, target) in enumerate((
-            (k_hbm, k_ref), (v_hbm, v_ref), (q_hbm, q_ref), (g_hbm, g_ref),
-            (doc_hbm, doc_ref), (logit_hbm, logit_ref),
-        ))
+        for i, source, target in (
+            (0, k_hbm, k_ref), (1, doc_hbm, doc_ref), (2, logit_hbm, logit_ref),
+            (3, v_hbm, v_ref), (3, q_hbm, q_ref), (3, g_hbm, g_ref),
+        )
     ]
-    for i in (0, 4, 5, 1, 2, 3):
-        loads[i].start()
+    for load in loads:
+        load.start()
 
     def peer(way, dist):
         return {"seq": lax.rem(me + signs[way] * dist + n, n)}
@@ -99,14 +100,14 @@
     def norm_copy(way, dist):
         return pltpu.make_async_remote_copy(
             src_ref=norm_src.at[way], dst_ref=norm_got.at[way, dist - 1],
-            send_sem=norm_send.at[way, dist - 1], recv_sem=norm_recv.at[way, dist - 1],
+            send_sem=norm_send.at[way], recv_sem=norm_recv.at[way],
             device_id=peer(way, dist), device_id_type=MESH,
         )
 
     def mem_copy(way, step, h):
         return pltpu.make_async_remote_copy(
             src_ref=mem_src.at[way, step, h], dst_ref=mem_got.at[way, step, h],
-            send_sem=mem_send.at[way, step], recv_sem=mem_recv.at[way, step, h],
+            send_sem=mem_send.at[way], recv_sem=mem_recv.at[way, step, h],
             device_id=peer(way, 1 << step), device_id_type=MESH,
         )
 
@@ -135,12 +136,22 @@
             def _():
                 norm_copy(way, dist).start()
 
+    def behind(way):
+        return me if way == 0 else n - 1 - me
+
+    def wait_norms(way, count, sem):
+        for some in range(1, reach + 1):
+            @pl.when(jnp.minimum(count, reach) == some)
+            def _():
+                space = norm_got.at[way, pl.ds(0, some)]
+                pltpu.make_async_copy(space, space, sem.at[way]).wait()
+
     def take_norms(way):
         norm_sum[way] = jnp.zeros_like(norm_sum[way])
+        wait_norms(way, behind(way), norm_recv)
         for dist in range(1, reach + 1):
             @pl.when(can_recv(way, dist))
             def _():
-                norm_copy(way, dist).wait_recv()
                 norm_sum[way] += weight(way, dist) * norm_got[way, dist - 1]
 
     def send_mem(way, step, h):
@@ -325,6 +336,10 @@
 
         return [rows_of(i) for i in range(blocks)]
 
+    def add_extra(h):
+        for i in range(blocks):
+            qo[part(i), cols(h)] += extra[part(i), cols(h)]
+
     def finish(h):
         hs = cols(h)
         local_share = 1.0 - share(h, size)
@@ -338,7 +353,6 @@
             ko[part(i), hs] = ko[part(i), hs] * scale + turned * k_slope[part(i), hs]
             value = dot_nn(jnp.concatenate([low, low], axis=1), below)
             vo[part(i), hs] = vo[part(i), hs] * local_share + value
-            qo[part(i), hs] += extra[part(i), hs]
 
     def key_memory(h):
         def run():
@@ -370,8 +384,9 @@
             kf[part(i), cols(h)] = low
             norm = norm + jnp.sum(low.astype(F32), axis=0, keepdims=True)
         norm_src[0, h:h + 1, :] = norm
-    for i in (4, 5, 1, 2, 3):
-        loads[i].wait()
+    loads[1].wait()
+    loads[2].wait()
+    pltpu.make_async_copy(held_ref, held_ref, load_sem.at[3]).wait()
     attend(-1, *(key_memory(h) for h in range(heads)), *(query_features(h) for h in range(heads)))
     pl.semaphore_wait(barrier, jnp.minimum(me, reach) + jnp.minimum(n - 1 - me, reach))
     send_norms(0)
@@ -383,8 +398,8 @@
     last = len(units) + 1
     early = steps == 2 and heads == 3 and blocks == 4
     if early:
-        polls = {6: [(0, 0, 0)], 8: [(0, 0, 1)], 9: [(0, 0, 2)], 10: [(0, 1, 0)], 11: [(0, 1, 1), (1, 0, 0)], 12: [(0, 1, 2)]}
-        reads = {11: [0], 13: [1, 2]}
+        polls = {6: [(0, 0, 0)], 7: [(0, 0, 1)], 8: [(0, 0, 2)], 11: [(0, 1, 0), (1, 0, 0)], 12: [(0, 1, 1), (0, 1, 2)]}
+        reads = {13: [0, 1, 2]}
         late = [(1, 0, 1), (1, 0, 2)]
     else:
         polls, reads = {}, {}
@@ -401,6 +416,8 @@
             take_norms(0)
             attend(-1, memory_grads(0))
             send_mem(1, 0, 0)
+        if at == last - 1:
+            attend(-1, local_gate(heads - 1))
         for way, step, h in polls.get(at, []):
             take_mem(way, step, h)
             if (way, step) == (0, steps - 1):
@@ -409,11 +426,10 @@
             if at == min(7 + 2 * turn, last):
                 hear(turn)
                 tell(turn + 1)
-        if at == last - 1:
-            attend(-1, local_gate(heads - 1))
-            if early:
-                send_gates()
-                take_mem(*late.pop(0))
+        if at == last - 1 and early:
+            send_gates()
+            way, step, h = late.pop(0)
+            take_mem(way, step, h)
     for h in range(last - begin + 1, heads):
         attend(-1, memory_grads(h))
         send_mem(1, 0, h)
@@ -429,22 +445,23 @@
         send_norms(1)
         send_gates()
     for h in range(heads):
+        add_extra(h)
+    share_o[...] = jnp.broadcast_to(1.0 - share(heads - 1, size), share_o.shape)
+    for h in range(heads - 1):
         take_mem(1, steps - 1, h)
         finish(h)
     for way in range(2):
-        for dist in range(1, reach + 1):
-            @pl.when(can_send(way, dist))
-            def _():
-                norm_copy(way, dist).wait_send()
-        for step in range(steps):
-            @pl.when(can_send(way, 1 << step))
-            def _():
-                pltpu.make_async_copy(mem_src.at[way, step], mem_src.at[way, step], mem_send.at[way, step]).wait()
+        ahead = behind(1 - way)
+        wait_norms(way, ahead, norm_send)
+        for some in range(1, steps + 1):
+            @pl.when((ahead >= 1 << (some - 1)) & ((ahead < 1 << some) | (some == steps)))
+            def _():
+                space = mem_src.at[way, pl.ds(0, some)]
+                pltpu.make_async_copy(space, space, mem_send.at[way]).wait()
+    take_mem(1, steps - 1, heads - 1)
+    later_o[...] = mem_sum[1, heads - 1]
     take_norms(1)
-    for h in range(heads):
-        norm = norm_sum[1, h:h + 1, :]
-        for i in range(blocks):
-            ko[part(i), cols(h)] += norm * k_slope[part(i), cols(h)]
+    norm_o[...] = norm_sum[1]
     others = gate_all.at[pl.ds(0, n - 1)]
     pltpu.make_async_copy(others, others, gate_recv).wait()
     gates = gate_all[0]
@@ -454,13 +471,42 @@
     pltpu.make_async_copy(others, others, gate_send).wait()
 
 
-def write(heads, q_ref, k_ref, v_ref, gate_ref, q_hbm, k_hbm, v_hbm, gate_o, sems):
-    copies = [
-        pltpu.make_async_copy(source, target, sems.at[i])
-        for i, (source, target) in enumerate(((q_ref, q_hbm), (k_ref, k_hbm), (v_ref, v_hbm)))
-    ]
-    for copy in copies:
-        copy.start()
+def write(
+    heads, size, block,
+    q_ref, k_ref, v_ref, gate_ref, later_ref, norm_ref, share_ref, slope_ref, kf_ref, held_ref,
+    q_hbm, k_hbm, v_hbm, gate_o, k_out, v_out, sems,
+):
+    rows = q_ref.shape[0]
+    ready = (heads - 1) * size
+    front, back = slice(0, ready), slice(ready, ready + size)
+    copies = []
+
+    def send(source, target):
+        copies.append(pltpu.make_async_copy(source, target, sems.at[len(copies)]))
+        copies[-1].start()
+
+    send(q_ref, q_hbm)
+    if ready:
+        send(v_ref.at[:, front], v_hbm.at[:, front])
+        for h in range(heads - 1):
+            hs = slice(h * size, (h + 1) * size)
+            for i in range(rows // block):
+                here = slice(i * block, (i + 1) * block)
+                k_out[here, hs] = k_ref[here, hs] + norm_ref[h:h + 1, :] * slope_ref[here, hs]
+        send(k_out.at[:, front], k_hbm.at[:, front])
+    high, rest = split(later_ref[...])
+    beside = jnp.concatenate([high, rest], axis=1)
+    below = jnp.concatenate([high, rest], axis=0)
+    for i in range(rows // block):
+        here = slice(i * block, (i + 1) * block)
+        v_i = held_ref[0, here, back]
+        low = kf_ref[here, back]
+        turned = dot_nt(jnp.concatenate([v_i, v_i], axis=1), beside) + norm_ref[heads - 1:heads, :]
+        k_out[here, back] = k_ref[here, back] * size ** -0.5 + turned * slope_ref[here, back]
+        value = dot_nn(jnp.concatenate([low, low], axis=1), below)
+        v_out[here, :] = v_ref[here, back] * share_ref[0:1, :] + value
+    send(k_out.at[:, back], k_hbm.at[:, back])
+    send(v_out, v_hbm.at[:, back])
     for h in range(heads):
         gate_o[h] = jnp.sum(gate_ref[h:h + 1, :])
     for copy in copies:
@@ -484,22 +530,21 @@
         hbm = pl.BlockSpec(memory_space=pltpu.HBM)
         tall = -(-heads // 8) * 8
         dma = pltpu.SemaphoreType.DMA
+        small = jax.ShapeDtypeStruct((tall, size), F32)
         local = pl.pallas_call(
             functools.partial(kernel, n, steps, reach, heads, size, block),
-            out_shape=(wide, wide, wide, jax.ShapeDtypeStruct((tall, size), F32)),
+            out_shape=(
+                wide, wide, wide, small, jax.ShapeDtypeStruct((size, size), F32), small, small, wide,
+                jax.ShapeDtypeStruct((rows, width), BF16), jax.ShapeDtypeStruct((3, rows, width), BF16),
+            ),
             in_specs=[hbm] * 6,
-            out_specs=(vmem,) * 4,
+            out_specs=(vmem,) * 10,
             scratch_shapes=[
                 pltpu.SMEM(doc_index.shape, jnp.int32),
                 pltpu.SMEM(gate_logit.shape, F32),
                 pltpu.VMEM((rows, width), BF16),
+                dma((4,)),
                 pltpu.VMEM((rows, width), BF16),
-                pltpu.VMEM((rows, width), BF16),
-                pltpu.VMEM((rows, width), BF16),
-                dma((6,)),
-                pltpu.VMEM((rows, width), BF16),
-                pltpu.VMEM((rows, width), BF16),
-                pltpu.VMEM((rows, width), F32),
                 pltpu.VMEM((rows, width), F32),
                 pltpu.VMEM((rows, width), F32),
                 pltpu.VMEM((heads, rows, size), F32),
@@ -514,9 +559,9 @@
                 pltpu.VMEM((2, steps, heads, size, size), F32),
                 pltpu.VMEM((2, steps, heads, size, size), F32),
                 pltpu.VMEM((2, heads, size, size), F32),
-                dma((2, reach)),
-                dma((2, reach)),
-                dma((2, steps)),
+                dma((2,)),
+                dma((2,)),
+                dma((2,)),
                 dma((2, steps, heads)),
                 dma(()),
                 dma(()),
@@ -532,11 +577,11 @@
             name="segment_backward",
         )(*(pltpu.with_memory_space_constraint(x, pltpu.HBM) for x in (doc_index, gate_logit, queries, key_vectors, value_vectors, out_grad)))
         return pl.pallas_call(
-            functools.partial(write, heads),
+            functools.partial(write, heads, size, block),
             out_shape=(wide, wide, wide, jax.ShapeDtypeStruct((heads,), F32)),
-            in_specs=[vmem] * 4,
+            in_specs=[vmem] * 10,
             out_specs=(hbm, hbm, hbm, smem),
-            scratch_shapes=[dma((3,))],
+            scratch_shapes=[pltpu.VMEM((rows, width), F32), pltpu.VMEM((rows, size), F32), dma((5,))],
             compiler_params=pltpu.CompilerParams(vmem_limit_bytes=16 * 1024 * 1024),
             cost_estimate=pl.CostEstimate(
                 flops=8 * rows * width * size, bytes_accessed=12 * rows * width,

time: 24.4 us -> 24 us (0.984)
  Pallas kernels: 23.6 us -> 23.2 us
    pallas_call x1, Pallas kernels: 20.9 us -> 20.4 us  [per_device(): pl.pallas_call(functools.partial(kernel, n, steps, reach, heads, size, bl...]
where the time goes in v5:
time: 24 us; the launch traced here: 23.8 us
  Pallas kernels  23.2 us (97%)
  between operations  0.64 us (3%)
    pallas_call x1, Pallas kernels, per_device(): pl.pallas_call(functools.partial(kernel, n, steps, reach, heads, size, bl...  20.4 us
    pallas_call x1, Pallas kernels, per_device(): pl.pallas_call(functools.partial(write, heads, size, block), out_shape=(w...  2.77 us

profile of v5, /device:TPU:0, one launch (start us, length us, event | category | flops | bytes accessed | tf_op | source)
XLA Modules:
  0.0 23.8 jit_solution(14615608638067865734)
XLA Ops:
  0.6 20.4 %segment_backward.1 = (f32[1024,384]{1,0:T(8,128)S(1)}, f32[1024,384]{1,0:T(8,128)S(1)}, f32[1024,384]{1,0:T(8,128)S(1)}, f32[8,128]{1,0:T(8,128)S(1)}, f32[128,...) custom-call(s32[8]{0:T(128)} %doc_hbm.1, ...), custom_call_target="tpu_custom_call" | custom-call | flops 5637144576 | bytes 7864320 | tf_op jit(solution)/shard_map/segment_backward/pallas_call | solution.py:534
  21.0 2.8 %segment_finish.1 = (f32[1024,384]{1,0:T(8,128)}, f32[1024,384]{1,0:T(8,128)}, f32[1024,384]{1,0:T(8,128)}, f32[3]{0:T(128)}) custom-call(f32[1024,384]{1,0:T(8,128)S(1)} %get-tuple-element.14.q_ref, f32[1024,384]{1,0:T(8,128)S(1)} %get-tuple-element.15.k_ref, f32[1024,384]{1,0:T(8,128)S(1)} %get-tuple-element.16.v_ref, ...), custom_call_target="tpu_custom_call" | custom-call | flops 402653184 | bytes 4718592 | tf_op jit(solution)/shard_map/segment_finish/pallas_call | solution.py:579

commit v6 on v5

--- a/solution.py
+++ b/solution.py
@@ -399,8 +399,7 @@
     early = steps == 2 and heads == 3 and blocks == 4
     if early:
         polls = {6: [(0, 0, 0)], 7: [(0, 0, 1)], 8: [(0, 0, 2)], 11: [(0, 1, 0), (1, 0, 0)], 12: [(0, 1, 1), (0, 1, 2)]}
-        reads = {13: [0, 1, 2]}
-        late = [(1, 0, 1), (1, 0, 2)]
+        reads, late = {}, []
     else:
         polls, reads = {}, {}
         late = [(way, step, h) for step in range(steps - 1) for h in range(heads) for way in range(2)]
@@ -415,6 +414,8 @@
         if at == begin:
             take_norms(0)
             attend(-1, memory_grads(0))
+            for way, step, h in polls.pop(at, []):
+                take_mem(way, step, h)
             send_mem(1, 0, 0)
         if at == last - 1:
             attend(-1, local_gate(heads - 1))
@@ -428,13 +429,13 @@
                 tell(turn + 1)
         if at == last - 1 and early:
             send_gates()
-            way, step, h = late.pop(0)
-            take_mem(way, step, h)
+            take_mem(1, 0, 1)
+            attend(-1, *(read_memory(h) for h in range(heads)))
+            send_norms(1)
+            take_mem(1, 0, 2)
     for h in range(last - begin + 1, heads):
         attend(-1, memory_grads(h))
         send_mem(1, 0, h)
-    if early:
-        send_norms(1)
     for way, step, h in late:
         take_mem(way, step, h)
     if not early:

time: 24 us -> 24 us (level)
  no operation moved by 1% of the time
where the time goes in v6:
time: 24 us; the launch traced here: 23.8 us
  Pallas kernels  23.2 us (97%)
  between operations  0.64 us (3%)
    pallas_call x1, Pallas kernels, per_device(): pl.pallas_call(functools.partial(kernel, n, steps, reach, heads, size, bl...  20.4 us
    pallas_call x1, Pallas kernels, per_device(): pl.pallas_call(functools.partial(write, heads, size, block), out_shape=(w...  2.77 us

profile of v6, /device:TPU:0, one launch (start us, length us, event | category | flops | bytes accessed | tf_op | source)
XLA Modules:
  0.0 23.8 jit_solution(3827000199917096587)
XLA Ops:
  0.6 20.4 %segment_backward.1 = (f32[1024,384]{1,0:T(8,128)S(1)}, f32[1024,384]{1,0:T(8,128)S(1)}, f32[1024,384]{1,0:T(8,128)S(1)}, f32[8,128]{1,0:T(8,128)S(1)}, f32[128,...) custom-call(s32[8]{0:T(128)} %doc_hbm.1, ...), custom_call_target="tpu_custom_call" | custom-call | flops 5637144576 | bytes 7864320 | tf_op jit(solution)/shard_map/segment_backward/pallas_call | solution.py:535
  21.0 2.8 %segment_finish.1 = (f32[1024,384]{1,0:T(8,128)}, f32[1024,384]{1,0:T(8,128)}, f32[1024,384]{1,0:T(8,128)}, f32[3]{0:T(128)}) custom-call(f32[1024,384]{1,0:T(8,128)S(1)} %get-tuple-element.14.q_ref, f32[1024,384]{1,0:T(8,128)S(1)} %get-tuple-element.15.k_ref, f32[1024,384]{1,0:T(8,128)S(1)} %get-tuple-element.16.v_ref, ...), custom_call_target="tpu_custom_call" | custom-call | flops 402653184 | bytes 4718592 | tf_op jit(solution)/shard_map/segment_finish/pallas_call | solution.py:580
